TPU v7x, 32 devices: a whole 2x2x4 slice. The times are simulated.
32 devices in a mesh: cluster: 4 (over x, core), leaf: 8 (over z, y).
Axes of the slice: x: 2, y: 2, z: 4, core: 2. Of those that a mesh axis runs over, the one named last changes fastest.
Arguments:
- probes: float32 [32768, 512], P(('cluster', 'leaf')), may hold values from -6 to 6
- dense_leaf: float32 [32768, 1024], P(('cluster', 'leaf')), may hold values from -0.1875 to 0.1875
- leaf_basis: float32 [32768, 128], P(('cluster', 'leaf')), may hold values from -0.1875 to 0.1875
- sibling_cores: float32 [32, 8, 128, 128], P(('cluster', 'leaf')), may hold values from -0.5 to 0.5
- transfer: float32 [32, 128, 128], P(('cluster', 'leaf')), may hold values from -0.5 to 0.5
- cluster_cores: float32 [4, 4, 128, 128], P('cluster'), may hold values from -0.1875 to 0.1875
Outputs:
- product: float32 [32768, 512], P(('cluster', 'leaf'))
All inputs are finite; a program needn't handle non-finite values.
Results may differ from a plain program's by a relative error of at most 0.00005.
Values sent between devices are 32-bit elements; how exact they have to be, the bound alone decides.
No kernel may reach another device: no remote copies, remote signals or barrier semaphores. Data moves between devices by JAX's collectives and lax.ppermute only.
A program may use at most 128 MiB of HBM per device.

v0:
```python
import jax
import jax.numpy as jnp
from jax import lax
from jax.sharding import PartitionSpec as P

HI = lax.Precision.HIGHEST


def local(probes, dense_leaf, leaf_basis, sibling_cores, transfer, cluster_cores):
    own = lax.axis_index("leaf")
    cown = lax.axis_index("cluster")
    cores = sibling_cores[0]
    trans = transfer[0]
    outer_cores = cluster_cores[0]
    rank_two = trans.shape[1]
    near = jnp.dot(dense_leaf, probes, precision=HI) + jnp.dot(dense_leaf.T, probes, precision=HI)
    coef = jnp.dot(leaf_basis.T, probes, precision=HI)
    turned = lax.all_to_all(cores, "leaf", split_axis=0, concat_axis=0, tiled=True)
    used = cores + jnp.transpose(turned, (0, 2, 1))
    piece = lax.all_gather(coef[None], "leaf", axis=0, tiled=True)
    count = piece.shape[0]
    block = used
    keep = (jnp.arange(count, dtype=jnp.int32) != own).astype(jnp.float32)
    block = block * keep[:, None, None]
    sib = jnp.einsum("jab,jbp->ap", block, piece, precision=HI)
    local_g = jnp.dot(trans.T, coef, precision=HI)
    nclu = outer_cores.shape[0]
    bkeep = (jnp.arange(nclu, dtype=jnp.int32) != cown).astype(jnp.float32)[:, None, None]
    masked = outer_cores * bkeep
    g_whole = lax.psum(local_g, "leaf")
    gathered = lax.all_gather(g_whole[None], "cluster", axis=0, tiled=True)
    front = jnp.einsum("dab,dbp->ap", masked, gathered, precision=HI)
    number = rank_two * lax.axis_size("cluster") // rank_two
    block = masked
    terms = jnp.einsum("dba,bp->dap", block, g_whole, precision=HI)
    field = front + lax.psum_scatter(
        terms.reshape(number * rank_two, g_whole.shape[1]),
        "cluster",
        scatter_dimension=0,
        tiled=True,
    )
    total = sib + jnp.dot(trans, field, precision=HI)
    return near + jnp.dot(leaf_basis, total, precision=HI)


def solution(mesh):
    return jax.shard_map(
        local,
        mesh=mesh,
        in_specs=(
            P(("cluster", "leaf"), None),
            P(("cluster", "leaf"), None),
            P(("cluster", "leaf"), None),
            P(("cluster", "leaf"), None, None, None),
            P(("cluster", "leaf"), None, None),
            P("cluster", None, None, None),
        ),
        out_specs=P(("cluster", "leaf"), None),
        check_vma=False,
    )
```

profile of v0, /device:TPU:0, one launch (start us, length us, event | category | flops | bytes accessed | tf_op | source)
XLA Modules:
  0.0 197.5 jit_solution(9313554170039844846)
XLA Ops:
  6.5 1.6 copy-done
  8.1 2.4 %fusion.10 = f32[128,512]{1,0:T(8,128)S(1)} fusion(f32[1024,128]{1,0:T(8,128)} %param.8, f32[1024,512]{1,0:T(8,128)S(1)} %copy-done), kind=kOutput, calls=%fused_computation.18 | convolution fusion | flops 805306368 | bytes 2883584 | tf_op jit(solution)/shard_map/dot_general | solution.py:17
  10.6 1.3 convolution_bitcast_fusion.3
  11.9 0.0 all-reduce.2.cloned.1.call-update
  11.9 0.0 all-gather.7.cloned.1.call-start
  11.9 73.8 %all-reduce.2.cloned.1.call-done = f32[128,512]{0,1:T(8,128)} async-done(((f32[128,512]{0,1:T(8,128)}), f32[128,512]{0,1:T(8,128)}) %all-reduce.2.cloned.1.call-update) | async-done | bytes 262160 | tf_op jit(solution)/shard_map/psum | solution.py:30
  85.8 0.0 reduce-scatter.2.cloned.1.call-start
  85.8 0.1 copy.10
  86.0 0.1 bitcast_multiply_fusion
  86.1 2.9 %fusion.11 = f32[512,512]{1,0:T(8,128)} fusion(f32[512,128]{1,0:T(8,128)S(1)} %bitcast.52, f32[128,512]{0,1:T(8,128)} %all-reduce.2.cloned.1.call-done), kind=kOutput, calls=%fused_computation.19 | convolution fusion | flops 402653184 | bytes 1572864 | tf_op jit(solution)/shard_map/dba,bp->dap/dot_general | solution.py:35
  89.0 0.0 reduce-scatter.2.cloned.1.call-update
  89.1 0.0 all-gather.5.cloned.1.call-start
  89.1 0.5 all-gather.5.cloned.1.call-update
  89.6 1.0 copy.9
  90.6 4.3 %all-to-all-start = ((f32[8,128,128]{1,2,0:T(8,128)}), f32[8,128,128]{1,2,0:T(8,128)}, u32[]{:S(2)}, u32[]{:S(2)}) async-start(f32[8,128,128]{1,2,0:T(8,128)} %copy.9), calls=%async_computation | async-start | bytes 1048576 | tf_op jit(solution)/shard_map/all_to_all | solution.py:18
  95.0 9.6 %fusion.8 = f32[1024,512]{1,0:T(8,128)} fusion(f32[1024,1024]{1,0:T(8,128)} %param.7, f32[1024,512]{1,0:T(8,128)S(1)} %copy-done), kind=kOutput, calls=%fused_computation.16 | convolution fusion | flops 6442450944 | bytes 8388608 | tf_op jit(solution)/shard_map/dot_general | solution.py:16
  104.6 9.6 %fusion.9 = f32[1024,512]{1,0:T(8,128)} fusion(f32[1024,1024]{1,0:T(8,128)} %param.7, f32[1024,512]{1,0:T(8,128)S(1)} %copy-done), kind=kOutput, calls=%fused_computation.17 | convolution fusion | flops 6442450944 | bytes 8388608 | tf_op jit(solution)/shard_map/dot_general | solution.py:16
  114.2 1.6 copy.14
  115.8 15.0 %reduce-scatter.2.cloned.1.call-done = f32[128,512]{1,0:T(8,128)} async-done(((f32[512,512]{1,0:T(8,128)}), f32[128,512]{1,0:T(8,128)}) %reduce-scatter.2.cloned.1.call-update) | async-done | bytes 262160 | tf_op jit(solution)/shard_map/reduce_scatter | solution.py:36
  130.7 2.4 %fusion.1 = f32[128,512]{1,0:T(8,128)} fusion(f32[128,512]{1,0:T(8,128)} %reduce-scatter.2.cloned.1.call-done, f32[4,128,128]{1,2,0:T(8,128)S(1)} %bitcast_multiply_fusion, f32[4,128,512]{2,1,0:T(8,128)S(1)} %bitcast.51), kind=kOutput, calls=%fused_computation.6 | convolution fusion | flops 402718720 | bytes 1835008 | tf_op jit(solution)/shard_map/dab,dbp->ap/dot_general | solution.py:32
  133.1 48.7 %all-gather.5.cloned.1.call-done = f32[1024,512]{1,0:T(8,128)} async-done(((f32[128,512]{1,0:T(8,128)}), f32[1024,512]{1,0:T(8,128)}) %all-gather.5.cloned.1.call-update) | async-done | bytes 2097168 | tf_op jit(solution)/shard_map/all_gather | solution.py:20
  181.8 3.4 %convolution_bitcast_fusion = f32[128,512]{1,0:T(8,128)S(1)} fusion(f32[8,128,512]{2,1,0:T(8,128)} %bitcast.53, f32[8,128,128]{1,2,0:T(8,128)} %all-to-all-done, f32[8]{0:T(128)S(1)} %compare_convert_fusion.1, f32[1,8,128,128]{3,2,1,0:T(8,128)} %param.9), kind=kOutput, calls=%fused_computation.1 | convolution fusion | flops 805568512 | bytes 3407904 | tf_op jit(solution)/shard_map/jab,jbp->ap/dot_general | solution.py:25
  185.2 1.3 fusion
  186.6 4.4 %bitcast_add_fusion = f32[1024,512]{1,0:T(8,128)} fusion(f32[1024,512]{1,0:T(8,128)S(1)} %copy-done.2, f32[1024,512]{1,0:T(8,128)S(1)} %copy-done.1, f32[128,512]{1,0:T(8,128)S(1)} %fusion, f32[1024,128]{1,0:T(8,128)} %param.8), kind=kOutput, calls=%fused_computation | convolution fusion | flops 806354944 | bytes 7077888 | tf_op jit(solution)/shard_map/dot_general | solution.py:43
  (19 shorter events, 0.1 us)
Async XLA Ops:
  6.5 1.6 copy-start
  6.5 4.0 %copy-start.6 = (f32[1,128,128]{2,1,0:T(8,128)S(1)}, f32[1,128,128]{2,1,0:T(8,128)}, u32[]{:S(2)}) copy-start(f32[1,128,128]{2,1,0:T(8,128)} %param.10) | copy-start | bytes 196612
  6.5 79.3 %copy-start.5 = (f32[1,4,128,128]{3,2,1,0:T(8,128)S(1)}, f32[1,4,128,128]{3,2,1,0:T(8,128)}, u32[]{:S(2)}) copy-start(f32[1,4,128,128]{3,2,1,0:T(8,128)} %param.11) | copy-start | bytes 786436
  6.5 79.2 %all-reduce.2.cloned.1.call-start = ((), (), s32[]{:S(2)}) async-start(), calls=%async_computation.2 | async-start | bytes 524288 | tf_op jit(solution)/shard_map/psum | solution.py:30
  10.5 78.5 %copy-start.3 = (f32[128,512]{1,0:T(8,128)}, f32[128,512]{1,0:T(8,128)S(1)}, u32[]{:S(2)}) copy-start(f32[128,512]{1,0:T(8,128)S(1)} %fusion.10) | copy-start | bytes 786436
  11.9 102.3 %all-gather.7.cloned.1.call-start = ((), (), s32[]{:S(2)}) async-start(), calls=%async_computation.5 | async-start | bytes 1310720 | tf_op jit(solution)/shard_map/all_gather | solution.py:31
  85.8 3.9 %copy-start.4 = (f32[1,8,128,128]{3,2,1,0:T(8,128)S(1)}, f32[1,8,128,128]{3,2,1,0:T(8,128)}, u32[]{:S(2)}) copy-start(f32[1,8,128,128]{3,2,1,0:T(8,128)} %param.9) | copy-start | bytes 1572868
  85.8 44.9 %reduce-scatter.2.cloned.1.call-start = ((), (), s32[]{:S(2)}) async-start(), calls=%async_computation.3 | async-start | bytes 1310720 | tf_op jit(solution)/shard_map/reduce_scatter | solution.py:36
  89.1 92.8 %all-gather.5.cloned.1.call-start = ((), (), s32[]{:S(2)}) async-start(), calls=%async_computation.4 | async-start | bytes 2359296 | tf_op jit(solution)/shard_map/all_gather | solution.py:20
  90.6 42.5 %all-to-all-start = ((f32[8,128,128]{1,2,0:T(8,128)}), f32[8,128,128]{1,2,0:T(8,128)}, u32[]{:S(2)}, u32[]{:S(2)}) async-start(f32[8,128,128]{1,2,0:T(8,128)} %copy.9), calls=%async_computation | async-start | bytes 1048576 | tf_op jit(solution)/shard_map/all_to_all | solution.py:18
  181.8 4.7 %copy-start.1 = (f32[1024,512]{1,0:T(8,128)S(1)}, f32[1024,512]{1,0:T(8,128)}, u32[]{:S(2)}) copy-start(f32[1024,512]{1,0:T(8,128)} %fusion.9) | copy-start | bytes 6291460
  181.8 4.7 %copy-start.2 = (f32[1024,512]{1,0:T(8,128)S(1)}, f32[1024,512]{1,0:T(8,128)}, u32[]{:S(2)}) copy-start(f32[1024,512]{1,0:T(8,128)} %fusion.8) | copy-start | bytes 6291460
Sparse Core Ops, SparseCore 0:
  12.0 73.7 all-reduce.1
  87.3 16.0 all-gather.6
  105.9 24.7 reduce-scatter.1
  132.7 49.0 all-gather.4
where the time goes:
time: 198 us; the launch traced here: 197 us
  waiting for transfers between devices  138 us (70%)
  matrix products  37.3 us (19%)
  between operations  13.3 us (7%)
  starting transfers between devices  4.44 us (2%)
  local copies, waits for them, and re-layouts  4.31 us (2%)
    psum x1, waiting for transfers between devices, local(): g_whole = lax.psum(local_g, 'leaf')  73.8 us
    all_gather x1, waiting for transfers between devices, local(): piece = lax.all_gather(coef[None], 'leaf', axis=0, tiled=True)  48.7 us
    reduce_scatter x1, waiting for transfers between devices, local(): lax.psum_scatter(terms.reshape(number * rank_two, g_whole.shape[1]), 'clu...  15 us
    dot_general x1, matrix products, local(): jnp.dot(dense_leaf.T, probes, precision=HI)  9.6 us
    dot_general x1, matrix products, local(): jnp.dot(dense_leaf, probes, precision=HI)  9.59 us
    dot_general x1, matrix products, local(): return near + jnp.dot(leaf_basis, total, precision=HI)  4.38 us
    all_to_all x1, starting transfers between devices, local(): lax.all_to_all(cores, 'leaf', split_axis=0, concat_axis=0, tiled=True)  4.32 us
  transfers between devices with their start and end apart: 5, of which 3 were waited for; matrix products, arithmetic and copies ran while one was open for 14% of the time, Pallas kernels for 0%

commit v1 on v0

--- a/solution.py
+++ b/solution.py
@@ -17,7 +17,9 @@
     coef = jnp.dot(leaf_basis.T, probes, precision=HI)
     turned = lax.all_to_all(cores, "leaf", split_axis=0, concat_axis=0, tiled=True)
     used = cores + jnp.transpose(turned, (0, 2, 1))
-    piece = lax.all_gather(coef[None], "leaf", axis=0, tiled=True)
+    piece = jnp.concatenate(
+        lax.all_to_all(jnp.stack([coef[None]] * lax.axis_size("leaf")), "leaf", 0, 0), axis=0
+    )
     count = piece.shape[0]
     block = used
     keep = (jnp.arange(count, dtype=jnp.int32) != own).astype(jnp.float32)

time: 198 us -> 162 us (0.82)
  waiting for transfers between devices: 138 us -> 96.7 us
  starting transfers between devices: 4.44 us -> 12 us
  matrix products: 37.3 us -> 34.1 us
    all_gather x1 -> x0, waiting for transfers between devices: 48.7 us -> none  [local(): piece = lax.all_gather(coef[None], 'leaf', axis=0, tiled=True)]
    all_to_all x0 -> x1, waiting for transfers between devices: none -> 5.45 us  [local(): lax.all_to_all(jnp.stack([coef[None]] * lax.axis_size('leaf')), 'leaf', 0...]
    all_to_all x0 -> x1, starting transfers between devices: none -> 4.47 us  [local(): lax.all_to_all(jnp.stack([coef[None]] * lax.axis_size('leaf')), 'leaf', 0...]
    all_to_all x1, starting transfers between devices: 4.32 us -> 7.44 us  [local(): lax.all_to_all(cores, 'leaf', split_axis=0, concat_axis=0, tiled=True)]
  transfers between devices with their start and end apart: 5 -> 5, of which waited for: 3 -> 3; matrix products, arithmetic and copies ran while one was open for 14% -> 18% of each run, Pallas kernels for 0% -> 0%
where the time goes in v1:
time: 162 us
  waiting for transfers between devices  96.7 us (60%)
  matrix products  34.1 us (21%)
  between operations  13.3 us (8%)
  starting transfers between devices  12 us (7%)
  local copies, waits for them, and re-layouts  5.6 us (3%)
    psum x1, waiting for transfers between devices, local(): g_whole = lax.psum(local_g, 'leaf')  74.3 us
    reduce_scatter x1, waiting for transfers between devices, local(): lax.psum_scatter(terms.reshape(number * rank_two, g_whole.shape[1]), 'clu...  16.9 us
    dot_general x1, matrix products, local(): jnp.dot(dense_leaf, probes, precision=HI)  9.76 us
    dot_general x1, matrix products, local(): jnp.dot(dense_leaf.T, probes, precision=HI)  8.12 us
    all_to_all x1, starting transfers between devices, local(): lax.all_to_all(cores, 'leaf', split_axis=0, concat_axis=0, tiled=True)  7.44 us
    all_to_all x1, waiting for transfers between devices, local(): lax.all_to_all(jnp.stack([coef[None]] * lax.axis_size('leaf')), 'leaf', 0...  5.45 us
    all_to_all x1, starting transfers between devices, local(): lax.all_to_all(jnp.stack([coef[None]] * lax.axis_size('leaf')), 'leaf', 0...  4.47 us
    dot_general x1, matrix products, local(): return near + jnp.dot(leaf_basis, total, precision=HI)  4.38 us
  transfers between devices with their start and end apart: 5, of which 3 were waited for; matrix products, arithmetic and copies ran while one was open for 18% of the time, Pallas kernels for 0%

profile of v1, /device:TPU:0, one launch (start us, length us, event | category | flops | bytes accessed | tf_op | source)
XLA Modules:
  0.0 161.8 jit_solution(14283489218369075645)
XLA Ops:
  6.5 2.2 %copy.9 = f32[8,128,128]{1,2,0:T(8,128)} copy(f32[8,128,128]{2,1,0:T(8,128)} %bitcast.56) | data formatting | bytes 1048576 | tf_op jit(solution)/shard_map/squeeze | solution.py:12
  8.7 7.4 %all-to-all-start = ((f32[8,128,128]{1,2,0:T(8,128)}), f32[8,128,128]{1,2,0:T(8,128)S(1)}, u32[]{:S(2)}, u32[]{:S(2)}) async-start(f32[8,128,128]{1,2,0:T(8,128)} %copy.9), calls=%async_computation | async-start | bytes 1048576 | tf_op jit(solution)/shard_map/all_to_all | solution.py:18
  16.2 0.0 all-reduce.2.cloned.1.call-start
  16.2 1.4 fusion.15
  17.6 1.3 convolution_bitcast_fusion.2
  18.9 0.0 all-reduce.2.cloned.1.call-update
  18.9 0.0 all-gather.3.cloned.1.call-start
  19.0 74.3 %all-reduce.2.cloned.1.call-done = f32[128,512]{0,1:T(8,128)} async-done(((f32[128,512]{0,1:T(8,128)}), f32[128,512]{0,1:T(8,128)}) %all-reduce.2.cloned.1.call-update) | async-done | bytes 262160 | tf_op jit(solution)/shard_map/psum | solution.py:32
  93.3 0.0 all-gather.3.cloned.1.call-update
  93.3 1.6 %stack.3 = f32[8,1,128,512]{3,2,1,0:T(8,128)} broadcast(f32[128,512]{1,0:T(8,128)S(1)} %fusion.15), dimensions={2,3} | broadcast | bytes 2359296 | tf_op jit(solution)/shard_map/stack | solution.py:21
  94.9 4.5 %all-to-all-start.1 = ((f32[8,1,128,512]{3,2,1,0:T(8,128)}), f32[8,1,128,512]{3,2,1,0:T(8,128)}, u32[]{:S(2)}, u32[]{:S(2)}) async-start(f32[8,1,128,512]{3,2,1,0:T(8,128)} %stack.3), calls=%async_computation.1 | async-start | bytes 4194304 | tf_op jit(solution)/shard_map/all_to_all | solution.py:21
  99.4 0.0 reduce-scatter.2.cloned.1.call-start
  99.5 0.1 copy.10
  99.6 0.1 bitcast_multiply_fusion
  99.7 2.0 %fusion.16 = f32[512,512]{1,0:T(8,128)} fusion(f32[512,128]{1,0:T(8,128)S(1)} %bitcast.55, f32[128,512]{0,1:T(8,128)S(1)} %copy-done.6), kind=kOutput, calls=%fused_computation.21 | convolution fusion | flops 402653184 | bytes 1572864 | tf_op jit(solution)/shard_map/dba,bp->dap/dot_general | solution.py:37
  101.8 9.8 %fusion.13 = f32[1024,512]{1,0:T(8,128)} fusion(f32[1024,1024]{1,0:T(8,128)} %param.7, f32[1024,512]{1,0:T(8,128)S(1)} %copy-done), kind=kOutput, calls=%fused_computation.18 | convolution fusion | flops 6442450944 | bytes 8388608 | tf_op jit(solution)/shard_map/dot_general | solution.py:16
  111.6 8.1 %fusion.14 = f32[1024,512]{1,0:T(8,128)} fusion(f32[1024,1024]{1,0:T(8,128)S(1)} %copy-done.1, f32[1024,512]{1,0:T(8,128)S(1)} %copy-done), kind=kOutput, calls=%fused_computation.19 | convolution fusion | flops 6442450944 | bytes 8388608 | tf_op jit(solution)/shard_map/dot_general | solution.py:16
  119.7 1.6 %copy.14 = f32[512,512]{1,0:T(8,128)S(1)} copy(f32[512,512]{0,1:T(8,128)} %all-gather.3.cloned.1.call-done) | data formatting | bytes 2097152 | tf_op jit(solution)/shard_map/all_gather | solution.py:33
  121.4 16.9 %reduce-scatter.2.cloned.1.call-done = f32[128,512]{1,0:T(8,128)} async-done(((f32[512,512]{1,0:T(8,128)}), f32[128,512]{1,0:T(8,128)}) %reduce-scatter.2.cloned.1.call-update) | async-done | bytes 262160 | tf_op jit(solution)/shard_map/reduce_scatter | solution.py:38
  138.2 2.4 %fusion.6 = f32[128,512]{1,0:T(8,128)} fusion(f32[128,512]{1,0:T(8,128)} %reduce-scatter.2.cloned.1.call-done, f32[4,128,128]{1,2,0:T(8,128)S(1)} %bitcast_multiply_fusion, f32[4,128,512]{2,1,0:T(8,128)S(1)} %bitcast.54), kind=kOutput, calls=%fused_computation.8 | convolution fusion | flops 402718720 | bytes 1835008 | tf_op jit(solution)/shard_map/dab,dbp->ap/dot_general | solution.py:34
  140.7 5.5 %all-to-all-done.1 = f32[8,1,128,512]{3,2,1,0:T(8,128)} async-done(((f32[8,1,128,512]{3,2,1,0:T(8,128)}), f32[8,1,128,512]{3,2,1,0:T(8,128)}, u32[]{:S(2)}, u32[]{:S(2)}) %all-to-all-start.1) | async-done | bytes 2097184 | tf_op jit(solution)/shard_map/all_to_all | solution.py:21
  146.1 3.4 %fusion.2 = f32[128,512]{1,0:T(8,128)S(1)} fusion(f32[8,1,128,512]{3,2,1,0:T(8,128)} %all-to-all-done.1, f32[8,128,128]{1,2,0:T(8,128)} %copy-done.5, f32[8]{0:T(128)S(1)} %compare_convert_fusion.1, f32[1,8,128,128]{3,2,1,0:T(8,128)} %param.9), kind=kOutput, calls=%fused_computation.3 | convolution fusion | flops 805568512 | bytes 3407904 | tf_op jit(solution)/shard_map/jab,jbp->ap/dot_general | solution.py:27
  149.5 1.3 fusion.5
  150.9 4.4 %bitcast_add_fusion = f32[1024,512]{1,0:T(8,128)} fusion(f32[1024,512]{1,0:T(8,128)S(1)} %copy-done.3, f32[1024,512]{1,0:T(8,128)S(1)} %copy-done.2, f32[128,512]{1,0:T(8,128)S(1)} %fusion.5, f32[1024,128]{1,0:T(8,128)} %param.8), kind=kOutput, calls=%fused_computation | convolution fusion | flops 806354944 | bytes 7077888 | tf_op jit(solution)/shard_map/dot_general | solution.py:45
  (23 shorter events, 0.1 us)
Async XLA Ops:
  6.5 9.7 %copy-start = (f32[1024,512]{1,0:T(8,128)S(1)}, f32[1024,512]{1,0:T(8,128)}, u32[]{:S(2)}) copy-start(f32[1024,512]{1,0:T(8,128)} %param.6) | copy-start | bytes 6291460
  6.5 9.7 %copy-start.4 = (f32[1024,128]{1,0:T(8,128)S(1)}, f32[1024,128]{1,0:T(8,128)}, u32[]{:S(2)}) copy-start(f32[1024,128]{1,0:T(8,128)} %param.8) | copy-start | bytes 1572868
  8.7 8.9 %copy-start.8 = (f32[1,128,128]{2,1,0:T(8,128)S(1)}, f32[1,128,128]{2,1,0:T(8,128)}, u32[]{:S(2)}) copy-start(f32[1,128,128]{2,1,0:T(8,128)} %param.10) | copy-start | bytes 196612
  8.7 84.6 %all-to-all-start = ((f32[8,128,128]{1,2,0:T(8,128)}), f32[8,128,128]{1,2,0:T(8,128)S(1)}, u32[]{:S(2)}, u32[]{:S(2)}) async-start(f32[8,128,128]{1,2,0:T(8,128)} %copy.9), calls=%async_computation | async-start | bytes 1048576 | tf_op jit(solution)/shard_map/all_to_all | solution.py:18
  16.2 77.1 %all-reduce.2.cloned.1.call-start = ((), (), s32[]{:S(2)}) async-start(), calls=%async_computation.3 | async-start | bytes 524288 | tf_op jit(solution)/shard_map/psum | solution.py:32
  18.9 100.8 %all-gather.3.cloned.1.call-start = ((), (), s32[]{:S(2)}) async-start(), calls=%async_computation.5 | async-start | bytes 1310720 | tf_op jit(solution)/shard_map/all_gather | solution.py:33
  93.3 1.6 %copy-start.5 = (f32[8,128,128]{1,2,0:T(8,128)}, f32[8,128,128]{1,2,0:T(8,128)S(1)}, u32[]{:S(2)}) copy-start(f32[8,128,128]{1,2,0:T(8,128)S(1)} %all-to-all-done) | copy-start | bytes 1572868
  94.9 4.5 %copy-start.7 = (f32[1,4,128,128]{3,2,1,0:T(8,128)S(1)}, f32[1,4,128,128]{3,2,1,0:T(8,128)}, u32[]{:S(2)}) copy-start(f32[1,4,128,128]{3,2,1,0:T(8,128)} %param.11) | copy-start | bytes 786436
  94.9 4.8 %copy-start.6 = (f32[128,512]{0,1:T(8,128)S(1)}, f32[128,512]{0,1:T(8,128)}, u32[]{:S(2)}) copy-start(f32[128,512]{0,1:T(8,128)} %all-reduce.2.cloned.1.call-done) | copy-start | bytes 786436
  94.9 51.2 %all-to-all-start.1 = ((f32[8,1,128,512]{3,2,1,0:T(8,128)}), f32[8,1,128,512]{3,2,1,0:T(8,128)}, u32[]{:S(2)}, u32[]{:S(2)}) async-start(f32[8,1,128,512]{3,2,1,0:T(8,128)} %stack.3), calls=%async_computation.1 | async-start | bytes 4194304 | tf_op jit(solution)/shard_map/all_to_all | solution.py:21
  99.4 38.8 %reduce-scatter.2.cloned.1.call-start = ((), (), s32[]{:S(2)}) async-start(), calls=%async_computation.4 | async-start | bytes 1310720 | tf_op jit(solution)/shard_map/reduce_scatter | solution.py:38
  101.8 9.8 %copy-start.1 = (f32[1024,1024]{1,0:T(8,128)S(1)}, f32[1024,1024]{1,0:T(8,128)}, u32[]{:S(2)}) copy-start(f32[1024,1024]{1,0:T(8,128)} %param.7) | copy-start | bytes 12582916
  146.1 4.7 %copy-start.2 = (f32[1024,512]{1,0:T(8,128)S(1)}, f32[1024,512]{1,0:T(8,128)}, u32[]{:S(2)}) copy-start(f32[1024,512]{1,0:T(8,128)} %fusion.14) | copy-start | bytes 6291460
  146.1 4.7 %copy-start.3 = (f32[1024,512]{1,0:T(8,128)S(1)}, f32[1024,512]{1,0:T(8,128)}, u32[]{:S(2)}) copy-start(f32[1024,512]{1,0:T(8,128)} %fusion.13) | copy-start | bytes 6291460
Sparse Core Ops, SparseCore 0:
  20.3 72.9 all-reduce.1
  94.8 16.0 all-gather.2
  113.4 24.7 reduce-scatter.1
